TPU v7x, 32 devices: a whole 2x2x4 slice. The times are simulated.
32 devices in a mesh: blk: 16 (over z, x, core), tp: 2 (over y).
Axes of the slice: x: 2, y: 2, z: 4, core: 2. Of those that a mesh axis runs over, the one named last changes fastest.
Arguments:
- weights: float32 [16, 1024, 1024], P('blk', None, 'tp'), may hold values from -6 to 6
- copies: bfloat16 [16, 1024, 1024], P('blk', None, 'tp'), may hold values from -60 to 60
- copies_mixed: bfloat16 [16, 1024, 1024], P('blk', None, 'tp'), may hold values from -64 to 64
- tracker: bfloat16 [16, 1024, 1024], P('blk', None, 'tp'), may hold values from -6 to 6
- tracker_copy: bfloat16 [16, 1024, 1024], P('blk', None, 'tp'), may hold values from -6 to 6
- tracker_mixed: bfloat16 [16, 1024, 1024], P('blk', None, 'tp'), may hold values from -6 to 6
- grad_prev: bfloat16 [16, 1024, 1024], P('blk', None, 'tp'), may hold values from -3 to 3
- tokens: bfloat16 [16, 1024, 1024], P('blk', 'tp'), may hold values from -12 to 12
- image_ids: int32 [16, 1024], P('blk'), may hold values from 0 to 5, never falling along the last dimension, each value on 1 to 197 neighbouring positions
- key_weight: bfloat16 [1024, 1024], P(None, 'tp'), may hold values from -0.1875 to 0.1875
- value_weight: bfloat16 [1024, 1024], P(None, 'tp'), may hold values from -0.1875 to 0.1875
- out_grad: bfloat16 [16, 1024, 1024], P('blk', None, 'tp'), may hold values from -48 to 48
- row_picks: int32 [16, 2, 64], replicated, may hold values from 0 to 1023, as said below
Outputs:
- weights_new: float32 [16, 1024, 1024], P('blk', None, 'tp')
- copies_new: bfloat16 [16, 1024, 1024], P('blk', None, 'tp')
- mixed_new: bfloat16 [16, 1024, 1024], P('blk', None, 'tp')
- tracker_new: bfloat16 [16, 1024, 1024], P('blk', None, 'tp')
- tracker_copy_new: bfloat16 [16, 1024, 1024], P('blk', None, 'tp')
- tracker_mixed_new: bfloat16 [16, 1024, 1024], P('blk', None, 'tp')
- grad_new: bfloat16 [16, 1024, 1024], P('blk', None, 'tp')
- consensus: float32 [], replicated
Inputs may be any that keep to these rules, and one draw needn't show every extreme that they name: `image_ids`: never falling along a replica's tokens; an image holds 1 to 197 tokens. `row_picks`: each row lists 64 different rows; the same picks serve every head shard of a replica.
All inputs are finite; a program needn't handle non-finite values.
Results may differ from a plain program's by a relative error of at most 0.0095.
The roundings to bfloat16 on the way count: a program that leaves them out, or rounds other values in their place, can miss the bound.
Values may be sent and summed in bfloat16 or wider, within the bound.
A program may use at most 128 MiB of HBM per device.

v0:
```python
import functools

import jax
import jax.numpy as jnp
from jax import lax
from jax.experimental import pallas as pl
from jax.experimental.pallas import tpu as pltpu
from jax.sharding import PartitionSpec as P

HD = 64
SEG_MOST = 197
TILE = 128

mixing_rate = 0.2
step_rate = 0.5

ANY = pl.BlockSpec(memory_space=pl.ANY)
VMEM = pl.BlockSpec(memory_space=pltpu.VMEM)


def contract(left, right, left_dim, right_dim):
    return lax.dot_general(
        left, right, (((left_dim,), (right_dim,)), ((), ())), preferred_element_type=jnp.float32
    )


def one_hot(picks, total_rows):
    columns = lax.broadcasted_iota(jnp.int32, (picks.shape[0], total_rows), 1)
    return (picks[:, None] == columns).astype(jnp.bfloat16)


def picked_rows(picks, total_rows):
    rows = lax.broadcasted_iota(jnp.int32, (total_rows, picks.shape[0]), 0)
    return jnp.any(rows == picks[None, :], axis=1, keepdims=True)


def replica_picks(row_picks, offset):
    count = lax.axis_size("blk")
    rank = lax.rem(lax.axis_index("blk") + offset + count, count)
    return lax.dynamic_index_in_dim(row_picks, rank, 0, keepdims=False)


def mix_stream(pieces, row_picks, stream, total_rows):
    picks = jnp.concatenate([replica_picks(row_picks, o)[stream] for o in (-1, 0, 1)], axis=0)
    values = jnp.concatenate(pieces, axis=0)
    return contract(one_hot(picks, total_rows), values, 0, 0) / 3.0


def gossip_kernel(
    blk_count, tp_count, values, part, lower, upper, total, slots, send_sem, recv_sem, part_sems
):
    blk, tp = lax.axis_index("blk"), lax.axis_index("tp")
    count = blk_count * tp_count
    me = blk * tp_count + tp
    mesh_type = pl.DeviceIdType.MESH
    barrier = pltpu.get_barrier_semaphore()

    def device(distance):
        flat = lax.rem(me + distance, count)
        return (flat // tp_count, lax.rem(flat, tp_count))

    def greet(distance, carry):
        pl.semaphore_signal(barrier, inc=1, device_id=device(distance), device_id_type=mesh_type)
        return carry

    lax.fori_loop(1, count, greet, 0)
    pl.semaphore_wait(barrier, count - 1)
    after = lax.rem(blk + 1, blk_count)
    before = lax.rem(blk + blk_count - 1, blk_count)
    up = pltpu.make_async_remote_copy(
        values, lower, send_sem.at[0], recv_sem.at[0], device_id=(after, tp), device_id_type=mesh_type
    )
    down = pltpu.make_async_remote_copy(
        values, upper, send_sem.at[1], recv_sem.at[1], device_id=(before, tp), device_id_type=mesh_type
    )
    up.start()
    down.start()

    def send(distance, carry):
        pltpu.make_async_remote_copy(
            part,
            slots.at[distance - 1],
            part_sems.at[0],
            part_sems.at[1],
            device_id=device(distance),
            device_id_type=mesh_type,
        ).start()
        return carry

    lax.fori_loop(1, count, send, 0)
    pltpu.make_async_copy(slots, slots, part_sems.at[1]).wait()
    pltpu.make_async_copy(slots, slots, part_sems.at[0]).wait()
    total[...] = jnp.sum(slots[...], axis=0) + part[...]
    up.wait()
    down.wait()


def gossip(values, part):
    blk_count, tp_count = lax.axis_size("blk"), lax.axis_size("tp")
    same = jax.ShapeDtypeStruct(values.shape, values.dtype)
    return pl.pallas_call(
        functools.partial(gossip_kernel, blk_count, tp_count),
        out_shape=(same, same, jax.ShapeDtypeStruct(part.shape, part.dtype)),
        in_specs=[VMEM, VMEM],
        out_specs=(VMEM, VMEM, VMEM),
        scratch_shapes=[
            pltpu.VMEM((blk_count * tp_count - 1,) + part.shape, part.dtype),
            pltpu.SemaphoreType.DMA((2,)),
            pltpu.SemaphoreType.DMA((2,)),
            pltpu.SemaphoreType.DMA((2,)),
        ],
        compiler_params=pltpu.CompilerParams(collective_id=0, has_side_effects=True),
        cost_estimate=pl.CostEstimate(flops=10000, bytes_accessed=10000000, transcendentals=0),
    )(values, part)


def gradient_kernel(count, *refs):
    pieces = refs[:count]
    (query_w, key_w, value_w, out_grad, ids_col, ids_row, picks_row, picks_col) = refs[count : count + 8]
    fields = refs[count + 8 : count + 12]
    grad_out, tracker_out, copy_out, kept = refs[count + 12 : count + 16]
    scratch = refs[count + 16 :]
    tok, qw, kw, vw, og, tr, tm, tc, gp, qs, ks, vs, qg, upd, bias, go, to, co, tok_sems, sems, out_sems = scratch
    total_rows, model_width = tok.shape
    width = qw.shape[1]
    rows_local = total_rows // count
    rank = lax.axis_index("tp")

    loads = []
    for shift in range(count):
        owner = lax.rem(rank - shift + count, count)
        where = pl.ds(pl.multiple_of(owner * rows_local, rows_local), rows_local)
        loads.append(pltpu.make_async_copy(pieces[shift], tok.at[where], tok_sems.at[shift]))
    sources = (query_w, key_w, value_w, out_grad) + fields
    for index, (source, target) in enumerate(zip(sources, (qw, kw, vw, og, tr, tm, tc, gp))):
        loads.append(pltpu.make_async_copy(source, target, sems.at[index]))
    for load in loads:
        load.start()
    for load in loads[: count + 3]:
        load.wait()

    proj = 256

    @pl.loop(0, total_rows // proj)
    def _(step):
        rows = pl.ds(pl.multiple_of(step * proj, proj), proj)
        block = tok[rows, :]
        query = jnp.dot(block, qw[...], preferred_element_type=jnp.float32).astype(jnp.bfloat16)
        qs[rows, :] = (query.astype(jnp.float32) * HD ** (-0.5)).astype(jnp.bfloat16)
        ks[rows, :] = jnp.dot(block, kw[...], preferred_element_type=jnp.float32).astype(jnp.bfloat16)
        vs[rows, :] = jnp.dot(block, vw[...], preferred_element_type=jnp.float32).astype(jnp.bfloat16)

    loads[count + 3].wait()
    pair = 2 * HD
    lane = lax.broadcasted_iota(jnp.int32, (1, pair), 1)
    first = jnp.where(lane < HD, 1.0, 0.0).astype(jnp.bfloat16)
    second = jnp.where(lane < HD, 0.0, 1.0).astype(jnp.bfloat16)
    reach = SEG_MOST - 1
    for low in range(0, total_rows, TILE):
        start = max(0, (low - reach) // TILE * TILE)
        end = min(total_rows, -(-(low + TILE + reach) // TILE) * TILE)
        span = end - start
        same = ids_col[low : low + TILE, :] == ids_row[:, start:end]
        tile_bias = jnp.where(same, 0.0, -1e30)
        bias[:TILE, :span] = tile_bias
        bias[TILE:, :span] = tile_bias

        @pl.loop(0, width // pair)
        def _(index):
            columns = pl.ds(pl.multiple_of(index * pair, pair), pair)
            query = qs[low : low + TILE, columns]
            outer = og[low : low + TILE, columns]
            keyed = ks[start:end, columns]
            valued = vs[start:end, columns]
            queries = jnp.concatenate([query * first, query * second], axis=0)
            outers = jnp.concatenate([outer * first, outer * second], axis=0)
            scores = contract(queries, keyed, 1, 1) + bias[:, :span]
            out_proj = contract(outers, valued, 1, 1)
            exponent = jnp.exp(scores - jnp.max(scores, axis=-1, keepdims=True))
            inverse = 1.0 / jnp.sum(exponent, axis=-1, keepdims=True)
            centre = jnp.sum(exponent * out_proj, axis=-1, keepdims=True) * inverse
            score_grad = (exponent * ((out_proj - centre) * (inverse * HD ** (-0.5)))).astype(
                jnp.bfloat16
            )
            both = jnp.dot(score_grad, keyed, preferred_element_type=jnp.float32)
            qg[low : low + TILE, columns] = jnp.where(lane < HD, both[:TILE], both[TILE:]).astype(
                jnp.bfloat16
            )

    for load in loads[count + 4 :]:
        load.wait()

    @pl.loop(0, model_width // TILE)
    def _(step):
        base = pl.multiple_of(step * TILE, TILE)
        rows = pl.ds(base, TILE)
        product = contract(tok[:, rows], qg[...], 0, 0)
        grad = (product * model_width ** (-0.5)).astype(jnp.bfloat16)
        copy = tc[rows, :].astype(jnp.float32)
        new = (
            tr[rows, :].astype(jnp.float32)
            + mixing_rate * (tm[rows, :].astype(jnp.float32) - copy)
            + grad.astype(jnp.float32)
            - gp[rows, :].astype(jnp.float32)
        ).astype(jnp.bfloat16)
        change = new.astype(jnp.float32) - copy
        index = lax.broadcasted_iota(jnp.int32, (TILE, picks_row.shape[1]), 0) + base
        hits = jnp.where(index == picks_row[...], 1.0, 0.0)
        picked = jnp.max(hits, axis=1, keepdims=True)
        go[rows, :] = grad
        to[rows, :] = new
        co[rows, :] = (copy + change * picked).astype(jnp.bfloat16)
        upd[rows, :] = change.astype(jnp.bfloat16)
        for slot, (source, target) in enumerate(((go, grad_out), (to, tracker_out), (co, copy_out))):
            pltpu.make_async_copy(source.at[rows], target.at[rows], out_sems.at[slot]).start()

    columns = lax.broadcasted_iota(jnp.int32, (picks_col.shape[0], model_width), 1)
    matrix = jnp.where(picks_col[...] == columns, 1.0, 0.0).astype(jnp.bfloat16)
    kept[...] = jnp.dot(matrix, upd[...], preferred_element_type=jnp.float32).astype(jnp.bfloat16)
    for slot, (source, target) in enumerate(((go, grad_out), (to, tracker_out), (co, copy_out))):
        pltpu.make_async_copy(source, target, out_sems.at[slot]).wait()


def gradient_stage(pieces, query_weight, key_weight, value_weight, out_grad, image_row, picks, fields):
    count = len(pieces)
    rows_local, model_width = pieces[0].shape
    total_rows = rows_local * count
    width = query_weight.shape[1]
    bf16 = jnp.bfloat16
    field = jax.ShapeDtypeStruct((model_width, width), bf16)
    span_most = min(total_rows, TILE + 2 * (-(-(SEG_MOST - 1) // TILE) * TILE))
    weight = pltpu.VMEM((model_width, width), bf16)
    row_block = pltpu.VMEM((total_rows, width), bf16)
    return pl.pallas_call(
        functools.partial(gradient_kernel, count),
        out_shape=(field, field, field, jax.ShapeDtypeStruct((picks.shape[0], width), bf16)),
        in_specs=[ANY] * (count + 4) + [VMEM] * 4 + [ANY] * 4,
        out_specs=(ANY, ANY, ANY, VMEM),
        scratch_shapes=[pltpu.VMEM((total_rows, model_width), bf16)]
        + [weight] * 3
        + [row_block]
        + [weight] * 4
        + [row_block] * 4
        + [weight, pltpu.VMEM((2 * TILE, span_most), jnp.float32)]
        + [weight] * 3
        + [
            pltpu.SemaphoreType.DMA((count,)),
            pltpu.SemaphoreType.DMA((8,)),
            pltpu.SemaphoreType.DMA((3,)),
        ],
        compiler_params=pltpu.CompilerParams(vmem_limit_bytes=56 * 2**20),
        cost_estimate=pl.CostEstimate(
            flops=8 * total_rows * model_width * width + 6 * total_rows * 640 * width,
            bytes_accessed=24 * model_width * width,
            transcendentals=total_rows * 640 * width // HD,
        ),
    )(
        *pieces,
        query_weight,
        key_weight,
        value_weight,
        out_grad,
        image_row.reshape(total_rows, 1),
        image_row.reshape(1, total_rows),
        picks.reshape(1, -1),
        picks.reshape(-1, 1),
        *fields,
    )


def per_device(
    weights,
    copies,
    copies_mixed,
    tracker,
    tracker_copy,
    tracker_mixed,
    grad_prev,
    tokens,
    image_ids,
    key_weight,
    value_weight,
    out_grad,
    row_picks,
):
    model_width = weights.shape[1]
    blk_count, tp_count = lax.axis_size("blk"), lax.axis_size("tp")
    pieces = [tokens[0]]
    for shift in range(1, tp_count):
        pieces.append(
            lax.ppermute(tokens[0], "tp", [(i, (i + shift) % tp_count) for i in range(tp_count)])
        )
    own_picks = replica_picks(row_picks, 0)
    copy_value = copies[0].astype(jnp.float32)
    mixed_value = copies_mixed[0].astype(jnp.float32)
    weights_new = (
        weights[0]
        + mixing_rate * (mixed_value - copy_value)
        - step_rate * tracker[0].astype(jnp.float32)
    )
    query_weight = (weights_new * model_width ** (-0.5)).astype(jnp.bfloat16)
    update = weights_new - copy_value
    picked = picked_rows(own_picks[0], model_width)
    copies_new = jnp.where(picked, copy_value + update, copy_value).astype(jnp.bfloat16)
    kept = contract(
        one_hot(own_picks[0], model_width), update.astype(jnp.bfloat16), 1, 0
    ).astype(jnp.bfloat16)
    up = [(i, (i + 1) % blk_count) for i in range(blk_count)]
    down = [(j, i) for i, j in up]
    lower = lax.ppermute(kept, "blk", up)
    upper = lax.ppermute(kept, "blk", down)
    mixed_new = (
        mixed_value + mix_stream([lower, kept, upper], row_picks, 0, model_width)
    ).astype(jnp.bfloat16)
    gap = mixed_new.astype(jnp.float32) - copies_new.astype(jnp.float32)
    part = jnp.broadcast_to(jnp.sum(gap * gap)[None, None], (8, 128))

    grad_new, tracker_new, tracker_copy_new, kept = gradient_stage(
        pieces,
        query_weight,
        key_weight,
        value_weight,
        out_grad[0],
        image_ids[0],
        own_picks[1],
        (tracker[0], tracker_mixed[0], tracker_copy[0], grad_prev[0]),
    )
    lower, upper, total = gossip(kept, part)
    tracker_mixed_new = (
        tracker_mixed[0].astype(jnp.float32)
        + mix_stream([lower, kept, upper], row_picks, 1, model_width)
    ).astype(jnp.bfloat16)
    entries = float(blk_count * model_width * model_width)
    return (
        weights_new[None],
        copies_new[None],
        mixed_new[None],
        tracker_new[None],
        tracker_copy_new[None],
        tracker_mixed_new[None],
        grad_new[None],
        total[0, 0] / entries,
    )


def solution(mesh):
    field = P("blk", None, "tp")
    return jax.shard_map(
        per_device,
        mesh=mesh,
        in_specs=(field,) * 7
        + (P("blk", "tp", None), P("blk", None), P(None, "tp"), P(None, "tp"), field, P()),
        out_specs=(field,) * 7 + (P(),),
        check_vma=False,
    )
```

profile of v0, /device:TPU:0, one launch (start us, length us, event | category | flops | bytes accessed | tf_op | source)
XLA Modules:
  0.0 87.6 jit_solution(451539731205043656)
XLA Ops:
  0.7 0.7 constant_dynamic-slice_fusion.1
  1.4 0.5 slice_bitcast_fusion.5
  1.9 0.0 copy-start.4
  1.9 0.0 copy-start
  1.9 0.0 copy-start.1
  1.9 3.5 %convolution_convert_fusion = bf16[64,512]{1,0:T(8,128)(2,1)S(1)} fusion(bf16[1,1024,512]{2,1,0:T(8,128)(2,1)} %param.14, s32[64]{0:T(128)S(1)} %get-tuple-element.34, bf16[1,1024,512]{2,1,0:T(8,128)(2,1)} %param.15, f32[1,1024,512]{2,1,0:T(8,128)} %param.13, bf16[1,1024,512]{2,1,0:T(8,128)(2,1)} %param.16), kind=kOutput, calls=%fused_computation.25 | convolution fusion | flops 72450048 | bytes 5308672 | tf_op jit(solution)/shard_map/dot_general | solution.py:22
  5.4 5.5 %collective-permute-start.1 = (bf16[64,512]{1,0:T(8,128)(2,1)S(1)}, bf16[64,512]{1,0:T(8,128)(2,1)S(1)}, u32[]{:S(2)}, u32[]{:S(2)}) collective-permute-start(bf16[64,512]{1,0:T(8,128)(2,1)S(1)} %convolution_convert_fusion), channel_id=1, source_target_pairs={{2,0},{4,2},{6,4},{8,6},{10,8},{12,10},{14,12},{16,14},{18,16},{20... | collective-permute-start | bytes 196616 | tf_op jit(solution)/shard_map/ppermute | solution.py:311
  10.9 0.0 collective-permute-start
  10.9 1.5 %collective-permute-start.2 = (bf16[512,1024]{1,0:T(8,128)(2,1)}, bf16[512,1024]{1,0:T(8,128)(2,1)}, u32[]{:S(2)}, u32[]{:S(2)}) collective-permute-start(bf16[512,1024]{1,0:T(8,128)(2,1)} %bitcast.8.refs_0_), channel_id=1, source_target_pairs={{0,1},{1,0},{2,3},{3,2},{4,5},{5,4},{6,7},{7,6},{8,9},{9,8},{10,11... | collective-permute-start | bytes 3145736 | tf_op jit(solution)/shard_map/ppermute | solution.py:291
  12.4 0.1 fusion.19
  12.5 0.7 copy.25.refs_9_
  13.2 0.0 copy-done.4
  13.2 1.1 %copy.24.refs_6_ = s32[1024,1]{1,0:T(8,128)} copy(s32[1024,1]{0,1:T(1,128)S(1)} %bitcast.104) | data formatting | bytes 8192 | tf_op jit(solution)/shard_map/reshape;squeeze | solution.py:263
  14.3 0.1 pad_add_fusion
  14.4 0.0 copy-done
  14.4 0.0 copy-done.1
  14.4 0.0 copy-start.2
  14.4 0.0 copy-start.3
  14.4 4.2 %fusion.13 = (bf16[1,1024,512]{2,1,0:T(8,128)(2,1)}, f32[1,1024,512]{2,1,0:T(8,128)}) fusion(bf16[1,1024,512]{2,1,0:T(8,128)(2,1)S(1)} %copy-done.1, pred[1024]{0:T(1024)(128)(4,1)S(1)} %fusion.19, bf16[1,1024,512]{2,1,0:T(8,128)(2,1)} %param.16, f32[1,1024,512]{2,1,0:T(8,128)S(1)} %copy-done, bf16[1,1024,512]{2,1,0:T(8,128)(2,1)} %param.15), kind=kLoop, calls=%fused_computation.19 | loop fusion | flops 6291456 | bytes 8389632 | tf_op jit(solution)/shard_map/convert_element_type | solution.py:304
  18.6 0.1 pad_add_fusion.1
  18.6 0.0 collective-permute-done.1
  18.6 0.0 collective-permute-done
  18.6 0.0 copy-done.2
  18.7 0.0 copy-done.3
  18.7 3.7 %multiply_reduce_fusion = (f32[]{:T(128)}, bf16[1024,512]{1,0:T(8,128)(2,1)}, bf16[1024,512]{1,0:T(8,128)(2,1)}) fusion(bf16[1,1024,512]{2,1,0:T(8,128)(2,1)S(1)} %copy-done.1, pred[1024]{0:T(1024)(128)(4,1)S(1)} %fusion.19, bf16[1,1024,512]{2,1,0:T(8,128)(2,1)S(1)} %copy-done.3, bf16[1,1024,512]{2,1,0:T(8,128)(2,1)S(1)} %copy-done.2, ...), kind=kOutput, calls=%fused_computation.21 | convolution fusion | flops 213647360 | bytes 7538436 | tf_op jit(solution)/shard_map/dot_general | solution.py:22
  22.3 11.6 %collective-permute-done.2.refs_1_ = bf16[512,1024]{1,0:T(8,128)(2,1)} collective-permute-done((bf16[512,1024]{1,0:T(8,128)(2,1)}, bf16[512,1024]{1,0:T(8,128)(2,1)}, u32[]{:S(2)}, u32[]{:S(2)}) %collective-permute-start.2) | collective-permute-done | bytes 1048608 | tf_op jit(solution)/shard_map/ppermute | solution.py:291
  34.0 0.0 copy-start.5
  34.0 35.6 %shard_map.188 = (bf16[1024,512]{1,0:T(8,128)(2,1)}, bf16[1024,512]{1,0:T(8,128)(2,1)}, bf16[1024,512]{1,0:T(8,128)(2,1)}, bf16[64,512]{1,0:T(8,128)(2,1)}) custom-call(bf16[512,1024]{1,0:T(8,128)(2,1)} %bitcast.8.refs_0_, bf16[512,1024]{1,0:T(8,128)(2,1)} %collective-permute-done.2.refs_1_, bf16[1024,512]{1,0:T(8,128)(2,1)} %get-tuple-element.25.refs_2_, ...), custom_call_target="tpu_custom_call" | custom-call | flops 6308233216 | bytes 12582912 | tf_op jit(solution)/shard_map/pallas_call | solution.py:234
  69.6 1.3 %broadcast_in_dim.41.part = f32[8,128]{1,0:T(8,128)} broadcast(f32[]{:T(128)} %get-tuple-element.24), dimensions={} | broadcast | bytes 4100 | tf_op jit(solution)/shard_map/broadcast_in_dim | solution.py:316
  70.9 11.2 %shard_map.189 = (bf16[64,512]{1,0:T(8,128)(2,1)}, bf16[64,512]{1,0:T(8,128)(2,1)}, f32[8,128]{1,0:T(8,128)}) custom-call(bf16[64,512]{1,0:T(8,128)(2,1)} %get-tuple-element.17.values, f32[8,128]{1,0:T(8,128)} %broadcast_in_dim.41.part), custom_call_target="tpu_custom_call" | custom-call | flops 10000 | bytes 10000000 | tf_op jit(solution)/shard_map/pallas_call | solution.py:101
  82.1 1.2 %slice.39 = f32[1,1]{1,0:T(1,128)} slice(f32[8,128]{1,0:T(8,128)} %get-tuple-element.21), slice={[0:1], [0:1]} | slice | bytes 8 | tf_op jit(solution)/shard_map/slice | solution.py:342
  84.0 0.0 copy-done.5
  84.0 2.5 %fusion.15 = bf16[1,1024,512]{2,1,0:T(8,128)(2,1)} fusion(s32[192]{0:T(256)S(1)} %pad_add_fusion.1, bf16[64,512]{1,0:T(8,128)(2,1)} %get-tuple-element.19, bf16[64,512]{1,0:T(8,128)(2,1)} %get-tuple-element.17.values, bf16[64,512]{1,0:T(8,128)(2,1)} %get-tuple-element.18, bf16[1,1024,512]{2,1,0:T(8,128)(2,1)S(1)} %copy-done.5), kind=kOutput, calls=%fused_computation.24 | convolution fusion | flops 204210176 | bytes 2294528 | tf_op jit(solution)/shard_map/dot_general | solution.py:22
  (1 shorter events, 0.0 us)
Async XLA Ops:
  1.9 11.3 %copy-start.4 = (s32[1,1024]{1,0:T(1,128)S(1)}, s32[1,1024]{1,0:T(1,128)}, u32[]{:S(2)}) copy-start(s32[1,1024]{1,0:T(1,128)} %refs_7_.1) | copy-start | bytes 12292
  1.9 12.5 %copy-start = (f32[1,1024,512]{2,1,0:T(8,128)S(1)}, f32[1,1024,512]{2,1,0:T(8,128)}, u32[]{:S(2)}) copy-start(f32[1,1024,512]{2,1,0:T(8,128)} %param.13) | copy-start | bytes 6291460
  1.9 12.5 %copy-start.1 = (bf16[1,1024,512]{2,1,0:T(8,128)(2,1)S(1)}, bf16[1,1024,512]{2,1,0:T(8,128)(2,1)}, u32[]{:S(2)}) copy-start(bf16[1,1024,512]{2,1,0:T(8,128)(2,1)} %param.14) | copy-start | bytes 3145732
  5.4 13.3 %collective-permute-start.1 = (bf16[64,512]{1,0:T(8,128)(2,1)S(1)}, bf16[64,512]{1,0:T(8,128)(2,1)S(1)}, u32[]{:S(2)}, u32[]{:S(2)}) collective-permute-start(bf16[64,512]{1,0:T(8,128)(2,1)S(1)} %convolution_convert_fusion), channel_id=1, source_target_pairs={{2,0},{4,2},{6,4},{8,6},{10,8},{12,10},{14,12},{16,14},{18,16},{20... | collective-permute-start | bytes 196616 | tf_op jit(solution)/shard_map/ppermute | solution.py:311
  10.9 7.8 %collective-permute-start = (bf16[64,512]{1,0:T(8,128)(2,1)S(1)}, bf16[64,512]{1,0:T(8,128)(2,1)S(1)}, u32[]{:S(2)}, u32[]{:S(2)}) collective-permute-start(bf16[64,512]{1,0:T(8,128)(2,1)S(1)} %convolution_convert_fusion), channel_id=1, source_target_pairs={{0,2},{2,4},{4,6},{6,8},{8,10},{10,12},{12,14},{14,16},{16,18},{18... | collective-permute-start | bytes 196616 | tf_op jit(solution)/shard_map/ppermute | solution.py:310
  10.9 23.1 %collective-permute-start.2 = (bf16[512,1024]{1,0:T(8,128)(2,1)}, bf16[512,1024]{1,0:T(8,128)(2,1)}, u32[]{:S(2)}, u32[]{:S(2)}) collective-permute-start(bf16[512,1024]{1,0:T(8,128)(2,1)} %bitcast.8.refs_0_), channel_id=1, source_target_pairs={{0,1},{1,0},{2,3},{3,2},{4,5},{5,4},{6,7},{7,6},{8,9},{9,8},{10,11... | collective-permute-start | bytes 3145736 | tf_op jit(solution)/shard_map/ppermute | solution.py:291
  14.4 4.3 %copy-start.2 = (bf16[1,1024,512]{2,1,0:T(8,128)(2,1)S(1)}, bf16[1,1024,512]{2,1,0:T(8,128)(2,1)}, u32[]{:S(2)}) copy-start(bf16[1,1024,512]{2,1,0:T(8,128)(2,1)} %param.15) | copy-start | bytes 3145732
  14.4 4.3 %copy-start.3 = (bf16[1,1024,512]{2,1,0:T(8,128)(2,1)S(1)}, bf16[1,1024,512]{2,1,0:T(8,128)(2,1)}, u32[]{:S(2)}) copy-start(bf16[1,1024,512]{2,1,0:T(8,128)(2,1)} %param.16) | copy-start | bytes 3145732
  34.0 50.0 %copy-start.5 = (bf16[1,1024,512]{2,1,0:T(8,128)(2,1)S(1)}, bf16[1,1024,512]{2,1,0:T(8,128)(2,1)}, u32[]{:S(2)}) copy-start(bf16[1,1024,512]{2,1,0:T(8,128)(2,1)} %param.18) | copy-start | bytes 3145732
where the time goes:
time: 87.9 us; the launch traced here: 87.6 us
  Pallas kernels  46.9 us (53%)
  waiting for transfers between devices  11.6 us (13%)
  matrix products  9.68 us (11%)
  starting transfers between devices  7.02 us (8%)
  local copies, waits for them, and re-layouts  5.51 us (6%)
  other arithmetic  4.43 us (5%)
  between operations  2.49 us (3%)
    pallas_call x1, Pallas kernels, gradient_stage(): pl.pallas_call(functools.partial(gradient_kernel, count), out_shape=(fiel...  35.6 us
    ppermute x1, waiting for transfers between devices, per_device(): lax.ppermute(tokens[0], 'tp', [(i, (i + shift) % tp_count) for i in range...  11.6 us
    pallas_call x1, Pallas kernels, gossip(): pl.pallas_call(functools.partial(gossip_kernel, blk_count, tp_count), out...  11.2 us
    dot_general x3, matrix products, contract(): lax.dot_general(left, right, (((left_dim,), (right_dim,)), ((), ())), pre...  9.68 us
    ppermute x1, starting transfers between devices, per_device(): upper = lax.ppermute(kept, 'blk', down)  5.49 us
    convert_element_type x1, other arithmetic, per_device(): jnp.where(picked, copy_value + update, copy_value).astype(jnp.bfloat16)  4.16 us
  transfers between devices with their start and end apart: 3, of which 1 were waited for; matrix products, arithmetic and copies ran while one was open for 11% of the time, Pallas kernels for 0%

commit v1 on v0

--- a/solution.py
+++ b/solution.py
@@ -114,49 +114,14 @@
     )(values, part)
 
 
-def gradient_kernel(count, *refs):
-    pieces = refs[:count]
-    (query_w, key_w, value_w, out_grad, ids_col, ids_row, picks_row, picks_col) = refs[count : count + 8]
-    fields = refs[count + 8 : count + 12]
-    grad_out, tracker_out, copy_out, kept = refs[count + 12 : count + 16]
-    scratch = refs[count + 16 :]
-    tok, qw, kw, vw, og, tr, tm, tc, gp, qs, ks, vs, qg, upd, bias, go, to, co, tok_sems, sems, out_sems = scratch
-    total_rows, model_width = tok.shape
-    width = qw.shape[1]
-    rows_local = total_rows // count
-    rank = lax.axis_index("tp")
-
-    loads = []
-    for shift in range(count):
-        owner = lax.rem(rank - shift + count, count)
-        where = pl.ds(pl.multiple_of(owner * rows_local, rows_local), rows_local)
-        loads.append(pltpu.make_async_copy(pieces[shift], tok.at[where], tok_sems.at[shift]))
-    sources = (query_w, key_w, value_w, out_grad) + fields
-    for index, (source, target) in enumerate(zip(sources, (qw, kw, vw, og, tr, tm, tc, gp))):
-        loads.append(pltpu.make_async_copy(source, target, sems.at[index]))
-    for load in loads:
-        load.start()
-    for load in loads[: count + 3]:
-        load.wait()
-
-    proj = 256
-
-    @pl.loop(0, total_rows // proj)
-    def _(step):
-        rows = pl.ds(pl.multiple_of(step * proj, proj), proj)
-        block = tok[rows, :]
-        query = jnp.dot(block, qw[...], preferred_element_type=jnp.float32).astype(jnp.bfloat16)
-        qs[rows, :] = (query.astype(jnp.float32) * HD ** (-0.5)).astype(jnp.bfloat16)
-        ks[rows, :] = jnp.dot(block, kw[...], preferred_element_type=jnp.float32).astype(jnp.bfloat16)
-        vs[rows, :] = jnp.dot(block, vw[...], preferred_element_type=jnp.float32).astype(jnp.bfloat16)
-
-    loads[count + 3].wait()
+def attend(lows, total_rows, qs, ks, vs, og, qg, ids_col, ids_row, bias):
+    width = qs.shape[1]
     pair = 2 * HD
     lane = lax.broadcasted_iota(jnp.int32, (1, pair), 1)
     first = jnp.where(lane < HD, 1.0, 0.0).astype(jnp.bfloat16)
     second = jnp.where(lane < HD, 0.0, 1.0).astype(jnp.bfloat16)
     reach = SEG_MOST - 1
-    for low in range(0, total_rows, TILE):
+    for low in lows:
         start = max(0, (low - reach) // TILE * TILE)
         end = min(total_rows, -(-(low + TILE + reach) // TILE) * TILE)
         span = end - start
@@ -165,7 +130,7 @@
         bias[:TILE, :span] = tile_bias
         bias[TILE:, :span] = tile_bias
 
-        @pl.loop(0, width // pair)
+        @pl.loop(0, width // pair, unroll=2 if width // pair % 2 == 0 else 1)
         def _(index):
             columns = pl.ds(pl.multiple_of(index * pair, pair), pair)
             query = qs[low : low + TILE, columns]
@@ -186,6 +151,140 @@
             qg[low : low + TILE, columns] = jnp.where(lane < HD, both[:TILE], both[TILE:]).astype(
                 jnp.bfloat16
             )
+
+
+def project(start, steps, tok, qw, kw, vw, qs, ks, vs, proj):
+    @pl.loop(0, steps)
+    def _(step):
+        rows = pl.ds(pl.multiple_of(start + step * proj, proj), proj)
+        block = tok[rows, :]
+        query = jnp.dot(block, qw[...], preferred_element_type=jnp.float32).astype(jnp.bfloat16)
+        qs[rows, :] = (query.astype(jnp.float32) * HD ** (-0.5)).astype(jnp.bfloat16)
+        ks[rows, :] = jnp.dot(block, kw[...], preferred_element_type=jnp.float32).astype(jnp.bfloat16)
+        vs[rows, :] = jnp.dot(block, vw[...], preferred_element_type=jnp.float32).astype(jnp.bfloat16)
+
+
+def piece_rows(index, rank, local, split, count):
+    if split:
+        half = local // 2
+        start = (rank * local, local - rank * half, (local + half) * (1 - rank))[index]
+        return pl.ds(pl.multiple_of(start, half), local if index == 0 else half)
+    start = lax.rem(rank - index + count, count) * local
+    return pl.ds(pl.multiple_of(start, local), local)
+
+
+def own_kernel(own, near, query_w, key_w, value_w, out_grad, ids_col, ids_row, done, *scratch):
+    tok, qw, kw, vw, og, qs, ks, vs, qg, bias, sems = scratch
+    total_rows = tok.shape[0]
+    local = own.shape[0]
+    half = local // 2
+    rank = lax.axis_index("tp")
+    own_rows = piece_rows(0, rank, local, True, 2)
+    targets = (
+        tok.at[own_rows],
+        tok.at[piece_rows(1, rank, local, True, 2)],
+        qw,
+        kw,
+        vw,
+        og,
+    )
+    loads = [
+        pltpu.make_async_copy(source, target, sems.at[index])
+        for index, (source, target) in enumerate(
+            zip((own, near, query_w, key_w, value_w, out_grad), targets)
+        )
+    ]
+    for load in loads:
+        load.start()
+    for load in loads:
+        load.wait()
+    project(rank * half, 3, tok, qw, kw, vw, qs, ks, vs, half)
+    for side in range(2):
+
+        @pl.when(rank == side)
+        def _():
+            lows = range(side * local, (side + 1) * local, TILE)
+            attend(lows, total_rows, qs, ks, vs, og, qg, ids_col, ids_row, bias)
+
+    done[...] = qg[own_rows, :]
+
+
+def own_stage(own, near, query_weight, key_weight, value_weight, out_grad, image_row):
+    local, model_width = own.shape
+    total_rows, width = out_grad.shape
+    bf16 = jnp.bfloat16
+    weight = pltpu.VMEM((model_width, width), bf16)
+    row_block = pltpu.VMEM((total_rows, width), bf16)
+    return pl.pallas_call(
+        own_kernel,
+        out_shape=jax.ShapeDtypeStruct((local, width), bf16),
+        in_specs=[ANY] * 6 + [VMEM] * 2,
+        out_specs=VMEM,
+        scratch_shapes=[pltpu.VMEM((total_rows, model_width), bf16)]
+        + [weight] * 3
+        + [row_block] * 5
+        + [pltpu.VMEM((2 * TILE, span_limit(total_rows)), jnp.float32)]
+        + [pltpu.SemaphoreType.DMA((6,))],
+        compiler_params=pltpu.CompilerParams(vmem_limit_bytes=40 * 2**20),
+        cost_estimate=pl.CostEstimate(
+            flops=4 * total_rows * model_width * width,
+            bytes_accessed=12 * model_width * width,
+            transcendentals=total_rows * 320 * width // HD,
+        ),
+    )(
+        own,
+        near,
+        query_weight,
+        key_weight,
+        value_weight,
+        out_grad,
+        image_row.reshape(total_rows, 1),
+        image_row.reshape(1, total_rows),
+    )
+
+
+def span_limit(total_rows):
+    return min(total_rows, TILE + 2 * (-(-(SEG_MOST - 1) // TILE) * TILE))
+
+
+def gradient_kernel(count, split, *refs):
+    pieces = refs[:count]
+    done, refs = (refs[count], refs[:count] + refs[count + 1 :]) if split else (None, refs)
+    (query_w, key_w, value_w, out_grad, ids_col, ids_row, picks_row, picks_col) = refs[count : count + 8]
+    fields = refs[count + 8 : count + 12]
+    grad_out, tracker_out, copy_out, kept = refs[count + 12 : count + 16]
+    scratch = refs[count + 16 :]
+    tok, qw, kw, vw, og, tr, tm, tc, gp, qs, ks, vs, qg, upd, bias, go, to, co, tok_sems, sems, out_sems = scratch
+    total_rows, model_width = tok.shape
+    rank = lax.axis_index("tp")
+
+    loads = []
+    for shift in range(count):
+        where = piece_rows(shift, rank, pieces[0].shape[0], split, count)
+        loads.append(pltpu.make_async_copy(pieces[shift], tok.at[where], tok_sems.at[shift]))
+    sources = (query_w, key_w, value_w, out_grad) + fields
+    for index, (source, target) in enumerate(zip(sources, (qw, kw, vw, og, tr, tm, tc, gp))):
+        loads.append(pltpu.make_async_copy(source, target, sems.at[index]))
+    if split:
+        own_rows = piece_rows(0, rank, pieces[0].shape[0], True, count)
+        loads.append(pltpu.make_async_copy(done, qg.at[own_rows], sems.at[8]))
+    for load in loads:
+        load.start()
+    for load in loads[: count + 4]:
+        load.wait()
+
+    project(0, total_rows // 256, tok, qw, kw, vw, qs, ks, vs, 256)
+    if split:
+        local = pieces[0].shape[0]
+        for side in range(2):
+
+            @pl.when(rank == side)
+            def _():
+                lows = range((1 - side) * local, (2 - side) * local, TILE)
+                attend(lows, total_rows, qs, ks, vs, og, qg, ids_col, ids_row, bias)
+
+    else:
+        attend(range(0, total_rows, TILE), total_rows, qs, ks, vs, og, qg, ids_col, ids_row, bias)
 
     for load in loads[count + 4 :]:
         load.wait()
@@ -221,31 +320,31 @@
         pltpu.make_async_copy(source, target, out_sems.at[slot]).wait()
 
 
-def gradient_stage(pieces, query_weight, key_weight, value_weight, out_grad, image_row, picks, fields):
+def gradient_stage(pieces, done, query_weight, key_weight, value_weight, out_grad, image_row, picks, fields):
     count = len(pieces)
-    rows_local, model_width = pieces[0].shape
-    total_rows = rows_local * count
+    model_width = pieces[0].shape[1]
+    total_rows = out_grad.shape[0]
+    extra = [] if done is None else [done]
     width = query_weight.shape[1]
     bf16 = jnp.bfloat16
     field = jax.ShapeDtypeStruct((model_width, width), bf16)
-    span_most = min(total_rows, TILE + 2 * (-(-(SEG_MOST - 1) // TILE) * TILE))
     weight = pltpu.VMEM((model_width, width), bf16)
     row_block = pltpu.VMEM((total_rows, width), bf16)
     return pl.pallas_call(
-        functools.partial(gradient_kernel, count),
+        functools.partial(gradient_kernel, count, done is not None),
         out_shape=(field, field, field, jax.ShapeDtypeStruct((picks.shape[0], width), bf16)),
-        in_specs=[ANY] * (count + 4) + [VMEM] * 4 + [ANY] * 4,
+        in_specs=[ANY] * (count + len(extra) + 4) + [VMEM] * 4 + [ANY] * 4,
         out_specs=(ANY, ANY, ANY, VMEM),
         scratch_shapes=[pltpu.VMEM((total_rows, model_width), bf16)]
         + [weight] * 3
         + [row_block]
         + [weight] * 4
         + [row_block] * 4
-        + [weight, pltpu.VMEM((2 * TILE, span_most), jnp.float32)]
+        + [weight, pltpu.VMEM((2 * TILE, span_limit(total_rows)), jnp.float32)]
         + [weight] * 3
         + [
             pltpu.SemaphoreType.DMA((count,)),
-            pltpu.SemaphoreType.DMA((8,)),
+            pltpu.SemaphoreType.DMA((9,)),
             pltpu.SemaphoreType.DMA((3,)),
         ],
         compiler_params=pltpu.CompilerParams(vmem_limit_bytes=56 * 2**20),
@@ -256,6 +355,7 @@
         ),
     )(
         *pieces,
+        *extra,
         query_weight,
         key_weight,
         value_weight,
@@ -268,7 +368,7 @@
     )
 
 
-def per_device(
+def device_step(
     weights,
     copies,
     copies_mixed,
@@ -285,11 +385,21 @@
 ):
     model_width = weights.shape[1]
     blk_count, tp_count = lax.axis_size("blk"), lax.axis_size("tp")
+    local = tokens.shape[1]
+    half = local // 2
+    split = tp_count == 2 and half % 256 == 0
     pieces = [tokens[0]]
-    for shift in range(1, tp_count):
-        pieces.append(
-            lax.ppermute(tokens[0], "tp", [(i, (i + shift) % tp_count) for i in range(tp_count)])
-        )
+    if split:
+        rank = lax.axis_index("tp")
+        swap = [(0, 1), (1, 0)]
+        first = lax.dynamic_slice_in_dim(tokens[0], (1 - rank) * half, half, 0)
+        pieces.append(lax.ppermute(first, "tp", swap))
+        later = lax.dynamic_slice_in_dim(tokens[0], rank * half, half, 0)
+        pieces.append(lax.ppermute(later, "tp", swap))
+    else:
+        for shift in range(1, tp_count):
+            hop = [(i, (i + shift) % tp_count) for i in range(tp_count)]
+            pieces.append(lax.ppermute(tokens[0], "tp", hop))
     own_picks = replica_picks(row_picks, 0)
     copy_value = copies[0].astype(jnp.float32)
     mixed_value = copies_mixed[0].astype(jnp.float32)
@@ -315,8 +425,15 @@
     gap = mixed_new.astype(jnp.float32) - copies_new.astype(jnp.float32)
     part = jnp.broadcast_to(jnp.sum(gap * gap)[None, None], (8, 128))
 
+    part, query_weight = lax.optimization_barrier((part, query_weight))
+    done = None
+    if split:
+        done = own_stage(
+            pieces[0], pieces[1], query_weight, key_weight, value_weight, out_grad[0], image_ids[0]
+        )
     grad_new, tracker_new, tracker_copy_new, kept = gradient_stage(
         pieces,
+        done,
         query_weight,
         key_weight,
         value_weight,
@@ -346,7 +463,7 @@
 def solution(mesh):
     field = P("blk", None, "tp")
     return jax.shard_map(
-        per_device,
+        device_step,
         mesh=mesh,
         in_specs=(field,) * 7
         + (P("blk", "tp", None), P("blk", None), P(None, "tp"), P(None, "tp"), field, P()),

time: 87.9 us -> 90.1 us (1.025)
  waiting for transfers between devices: 11.6 us -> 8.57 us
  Pallas kernels: 46.9 us -> 48.5 us
  matrix products: 9.68 us -> 11.1 us
  local copies, waits for them, and re-layouts: 5.51 us -> 6.47 us
    ppermute x3 -> x4, waiting for transfers between devices: 11.6 us -> 8.57 us  [the longest x1 8.56 us: device_step(): pieces.append(lax.ppermute(first, 'tp', swap))]
    pallas_call x1 -> x2, Pallas kernels: 35.6 us -> 37.3 us  [the longest x1 23.9 us: gradient_stage(): pl.pallas_call(functools.partial(gradient_kernel, count, done is not None...]
    dot_general x3, matrix products: 9.68 us -> 11.1 us  [contract(): lax.dot_general(left, right, (((left_dim,), (right_dim,)), ((), ())), pre...]
    dynamic_slice x0 -> x1, local copies, waits for them, and re-layouts: none -> 1.03 us  [device_step(): later = lax.dynamic_slice_in_dim(tokens[0], rank * half, half, 0)]
    ppermute x3 -> x4, starting transfers between devices: 7.02 us -> 7.53 us  [the longest x1 5.5 us: device_step(): upper = lax.ppermute(kept, 'blk', down)]
  transfers between devices with their start and end apart: 3 -> 4, of which waited for: 1 -> 1; matrix products, arithmetic and copies ran while one was open for 11% -> 15% of each run, Pallas kernels for 0% -> 15%
where the time goes in v1:
time: 90.1 us; the launch traced here: 89.7 us
  Pallas kernels  48.5 us (54%)
  matrix products  11.1 us (12%)
  waiting for transfers between devices  8.57 us (10%)
  starting transfers between devices  7.53 us (8%)
  local copies, waits for them, and re-layouts  6.47 us (7%)
  other arithmetic  4.94 us (5%)
  between operations  2.6 us (3%)
    pallas_call x1, Pallas kernels, gradient_stage(): pl.pallas_call(functools.partial(gradient_kernel, count, done is not None...  23.9 us
    pallas_call x1, Pallas kernels, own_stage(): pl.pallas_call(own_kernel, out_shape=jax.ShapeDtypeStruct((local, width),...  13.4 us
    pallas_call x1, Pallas kernels, gossip(): pl.pallas_call(functools.partial(gossip_kernel, blk_count, tp_count), out...  11.2 us
    dot_general x3, matrix products, contract(): lax.dot_general(left, right, (((left_dim,), (right_dim,)), ((), ())), pre...  11.1 us
    ppermute x1, waiting for transfers between devices, device_step(): pieces.append(lax.ppermute(first, 'tp', swap))  8.56 us
    ppermute x1, starting transfers between devices, device_step(): upper = lax.ppermute(kept, 'blk', down)  5.5 us
    convert_element_type x1, other arithmetic, device_step(): jnp.where(picked, copy_value + update, copy_value).astype(jnp.bfloat16)  4.67 us
  transfers between devices with their start and end apart: 4, of which 1 were waited for; matrix products, arithmetic and copies ran while one was open for 15% of the time, Pallas kernels for 15%

profile of v1, /device:TPU:0, one launch (start us, length us, event | category | flops | bytes accessed | tf_op | source)
XLA Modules:
  0.0 89.7 jit_solution(5736021632872125491)
XLA Ops:
  0.7 0.7 constant_dynamic-slice_fusion.1
  1.4 0.5 slice_bitcast_fusion.5
  1.9 0.0 copy-start
  1.9 3.4 %convolution_convert_fusion = bf16[64,512]{1,0:T(8,128)(2,1)S(1)} fusion(bf16[1,1024,512]{2,1,0:T(8,128)(2,1)} %param.14, s32[64]{0:T(128)S(1)} %get-tuple-element.40, bf16[1,1024,512]{2,1,0:T(8,128)(2,1)} %param.15, f32[1,1024,512]{2,1,0:T(8,128)} %param.13, bf16[1,1024,512]{2,1,0:T(8,128)(2,1)} %param.16), kind=kOutput, calls=%fused_computation.25 | convolution fusion | flops 72450048 | bytes 5308672 | tf_op jit(solution)/shard_map/dot_general | solution.py:22
  5.3 0.0 copy-start.9
  5.3 5.5 %collective-permute-start.1 = (bf16[64,512]{1,0:T(8,128)(2,1)S(1)}, bf16[64,512]{1,0:T(8,128)(2,1)S(1)}, u32[]{:S(2)}, u32[]{:S(2)}) collective-permute-start(bf16[64,512]{1,0:T(8,128)(2,1)S(1)} %convolution_convert_fusion), channel_id=1, source_target_pairs={{2,0},{4,2},{6,4},{8,6},{10,8},{12,10},{14,12},{16,14},{18,16},{20... | collective-permute-start | bytes 196616 | tf_op jit(solution)/shard_map/ppermute | solution.py:421
  10.8 0.0 collective-permute-start
  10.8 0.0 copy-done
  10.8 1.0 %dynamic-slice_bitcast_fusion = (bf16[256,1024]{1,0:T(8,128)(2,1)}, bf16[256,1024]{1,0:T(8,128)(2,1)}) fusion(bf16[1,512,1024]{2,1,0:T(8,128)(2,1)S(1)} %copy-done, s32[]{:T(128)S(6)} %select_n.32, s32[]{:T(128)S(6)} %select_n.31), kind=kLoop, calls=%fused_computation.28 | loop fusion | bytes 2097160 | tf_op jit(solution)/shard_map/dynamic_slice | solution.py:397
  11.9 1.5 %collective-permute-start.3 = (bf16[256,1024]{1,0:T(8,128)(2,1)}, bf16[256,1024]{1,0:T(8,128)(2,1)}, u32[]{:S(2)}, u32[]{:S(2)}) collective-permute-start(bf16[256,1024]{1,0:T(8,128)(2,1)} %get-tuple-element.30), channel_id=1, source_target_pairs={{0,1},{1,0},{2,3},{3,2},{4,5},{5,4},{6,7},{7,6},{8,9},{9,8},{10,11... | collective-permute-start | bytes 1572872 | tf_op jit(solution)/shard_map/ppermute | solution.py:398
  13.4 0.5 collective-permute-start.2
  13.9 0.1 fusion.19
  14.0 0.0 copy-done.9
  14.0 0.0 copy-start.2
  14.0 4.7 %fusion.13 = (bf16[1,1024,512]{2,1,0:T(8,128)(2,1)}, f32[1,1024,512]{2,1,0:T(8,128)}) fusion(bf16[1,1024,512]{2,1,0:T(8,128)(2,1)S(1)} %copy-done.9, pred[1024]{0:T(1024)(128)(4,1)S(1)} %fusion.19, bf16[1,1024,512]{2,1,0:T(8,128)(2,1)} %param.16, f32[1,1024,512]{2,1,0:T(8,128)} %param.13, bf16[1,1024,512]{2,1,0:T(8,128)(2,1)} %param.15), kind=kLoop, calls=%fused_computation.19 | loop fusion | flops 6291456 | bytes 8389632 | tf_op jit(solution)/shard_map/convert_element_type | solution.py:414
  18.7 0.1 pad_add_fusion
  18.8 0.1 pad_add_fusion.1
  18.9 0.7 copy.27.refs_11_
  19.6 0.0 copy-done.2
  19.6 0.2 copy.25.ids_col.refs_8_
  19.8 0.0 copy-start.1
  19.8 0.0 copy-start.3
  19.8 0.0 copy-start.4
  19.8 0.0 copy-start.5
  19.8 0.0 collective-permute-done.1
  19.9 0.0 collective-permute-done
  19.9 5.2 %multiply_convert_fusion = (bf16[1024,512]{1,0:T(8,128)(2,1)S(1)}, f32[]{:T(128)}, bf16[1024,512]{1,0:T(8,128)(2,1)}) fusion(bf16[1,1024,512]{2,1,0:T(8,128)(2,1)} %param.16, bf16[1,1024,512]{2,1,0:T(8,128)(2,1)S(1)} %copy-done.9, bf16[1,1024,512]{2,1,0:T(8,128)(2,1)} %param.15, f32[1,1024,512]{2,1,0:T(8,128)} %param.13, pred[1024]{0:T(1024)(128)(4,1)S(1)} %fusion.19, ...), kind=kOutput, calls=%fused_computation.21 | convolution fusion | flops 213647360 | bytes 7538436 | tf_op jit(solution)/shard_map/dot_general | solution.py:22
  25.0 0.0 copy-start.7
  25.1 1.2 %broadcast_in_dim.39.part = f32[8,128]{1,0:T(8,128)} broadcast(f32[]{:T(128)} %get-tuple-element.29), dimensions={} | broadcast | bytes 4100 | tf_op jit(solution)/shard_map/broadcast_in_dim | solution.py:426
  26.3 8.6 %collective-permute-done.2.near.refs_1_ = bf16[256,1024]{1,0:T(8,128)(2,1)S(1)} collective-permute-done((bf16[256,1024]{1,0:T(8,128)(2,1)}, bf16[256,1024]{1,0:T(8,128)(2,1)S(1)}, u32[]{:S(2)}, u32[]{:S(2)}) %collective-permute-start.2) | collective-permute-done | bytes 524320 | tf_op jit(solution)/shard_map/ppermute | solution.py:396
  34.9 0.0 copy-start.6
  34.9 0.0 copy-done.1
  34.9 0.0 copy-done.3
  34.9 0.0 copy-done.4
  34.9 0.0 copy-done.5
  34.9 13.4 %shard_map.188.refs_3_ = bf16[512,512]{1,0:T(8,128)(2,1)S(1)} custom-call(bf16[512,1024]{1,0:T(8,128)(2,1)S(1)} %bitcast.108, bf16[256,1024]{1,0:T(8,128)(2,1)S(1)} %collective-permute-done.2.near.refs_1_, bf16[1024,512]{1,0:T(8,128)(2,1)S(1)} %get-tuple-element.17.query_w.refs_4_, bf16[1024,512]{1,0:T(8,128)(2,1)S(1)} %copy-done.3, ...), custom_call_target="tpu_custom_call" | custom-call | flops 2147483648 | bytes 6291456 | tf_op jit(solution)/shard_map/pallas_call | solution.py:218
  48.2 0.0 copy-done.7
  48.2 0.0 copy-done.6
  48.3 0.0 copy-start.8
  48.3 0.8 copy-done.8
  49.1 0.0 collective-permute-done.3.refs_2_
  49.1 0.0 copy-start.10
  49.1 23.9 %shard_map.189 = (bf16[1024,512]{1,0:T(8,128)(2,1)}, bf16[1024,512]{1,0:T(8,128)(2,1)}, bf16[1024,512]{1,0:T(8,128)(2,1)}, bf16[64,512]{1,0:T(8,128)(2,1)}) custom-call(bf16[512,1024]{1,0:T(8,128)(2,1)} %bitcast.107, bf16[256,1024]{1,0:T(8,128)(2,1)} %copy-done.6, bf16[256,1024]{1,0:T(8,128)(2,1)} %collective-permute-done.3.refs_2_, ...), custom_call_target="tpu_custom_call" | custom-call | flops 6308233216 | bytes 12582912 | tf_op jit(solution)/shard_map/pallas_call | solution.py:333
  73.0 11.2 %shard_map.190 = (bf16[64,512]{1,0:T(8,128)(2,1)}, bf16[64,512]{1,0:T(8,128)(2,1)}, f32[8,128]{1,0:T(8,128)}) custom-call(bf16[64,512]{1,0:T(8,128)(2,1)} %get-tuple-element.20.values, f32[8,128]{1,0:T(8,128)} %broadcast_in_dim.39.part), custom_call_target="tpu_custom_call" | custom-call | flops 10000 | bytes 10000000 | tf_op jit(solution)/shard_map/pallas_call | solution.py:101
  84.3 1.2 %slice.39 = f32[1,1]{1,0:T(1,128)} slice(f32[8,128]{1,0:T(8,128)} %get-tuple-element.25), slice={[0:1], [0:1]} | slice | bytes 8 | tf_op jit(solution)/shard_map/slice | solution.py:459
  86.1 0.0 copy-done.10
  86.1 2.5 %fusion.15 = bf16[1,1024,512]{2,1,0:T(8,128)(2,1)} fusion(s32[192]{0:T(256)S(1)} %pad_add_fusion.1, bf16[64,512]{1,0:T(8,128)(2,1)} %get-tuple-element.23, bf16[64,512]{1,0:T(8,128)(2,1)} %get-tuple-element.20.values, bf16[64,512]{1,0:T(8,128)(2,1)} %get-tuple-element.22, bf16[1,1024,512]{2,1,0:T(8,128)(2,1)S(1)} %copy-done.10), kind=kOutput, calls=%fused_computation.24 | convolution fusion | flops 204210176 | bytes 2294528 | tf_op jit(solution)/shard_map/dot_general | solution.py:22
  (1 shorter events, 0.0 us)
Async XLA Ops:
  1.9 8.9 %copy-start = (bf16[1,512,1024]{2,1,0:T(8,128)(2,1)S(1)}, bf16[1,512,1024]{2,1,0:T(8,128)(2,1)}, u32[]{:S(2)}) copy-start(bf16[1,512,1024]{2,1,0:T(8,128)(2,1)} %param.20) | copy-start | bytes 3145732
  5.3 8.7 %copy-start.9 = (bf16[1,1024,512]{2,1,0:T(8,128)(2,1)S(1)}, bf16[1,1024,512]{2,1,0:T(8,128)(2,1)}, u32[]{:S(2)}) copy-start(bf16[1,1024,512]{2,1,0:T(8,128)(2,1)} %param.14) | copy-start | bytes 3145732
  5.3 14.5 %collective-permute-start.1 = (bf16[64,512]{1,0:T(8,128)(2,1)S(1)}, bf16[64,512]{1,0:T(8,128)(2,1)S(1)}, u32[]{:S(2)}, u32[]{:S(2)}) collective-permute-start(bf16[64,512]{1,0:T(8,128)(2,1)S(1)} %convolution_convert_fusion), channel_id=1, source_target_pairs={{2,0},{4,2},{6,4},{8,6},{10,8},{12,10},{14,12},{16,14},{18,16},{20... | collective-permute-start | bytes 196616 | tf_op jit(solution)/shard_map/ppermute | solution.py:421
  10.8 9.0 %collective-permute-start = (bf16[64,512]{1,0:T(8,128)(2,1)S(1)}, bf16[64,512]{1,0:T(8,128)(2,1)S(1)}, u32[]{:S(2)}, u32[]{:S(2)}) collective-permute-start(bf16[64,512]{1,0:T(8,128)(2,1)S(1)} %convolution_convert_fusion), channel_id=1, source_target_pairs={{0,2},{2,4},{4,6},{6,8},{8,10},{10,12},{12,14},{14,16},{16,18},{18... | collective-permute-start | bytes 196616 | tf_op jit(solution)/shard_map/ppermute | solution.py:420
  11.9 37.2 %collective-permute-start.3 = (bf16[256,1024]{1,0:T(8,128)(2,1)}, bf16[256,1024]{1,0:T(8,128)(2,1)}, u32[]{:S(2)}, u32[]{:S(2)}) collective-permute-start(bf16[256,1024]{1,0:T(8,128)(2,1)} %get-tuple-element.30), channel_id=1, source_target_pairs={{0,1},{1,0},{2,3},{3,2},{4,5},{5,4},{6,7},{7,6},{8,9},{9,8},{10,11... | collective-permute-start | bytes 1572872 | tf_op jit(solution)/shard_map/ppermute | solution.py:398
  13.4 21.5 %collective-permute-start.2 = (bf16[256,1024]{1,0:T(8,128)(2,1)}, bf16[256,1024]{1,0:T(8,128)(2,1)S(1)}, u32[]{:S(2)}, u32[]{:S(2)}) collective-permute-start(bf16[256,1024]{1,0:T(8,128)(2,1)} %get-tuple-element.31), channel_id=1, source_target_pairs={{0,1},{1,0},{2,3},{3,2},{4,5},{5,4},{6,7},{7,6},{8,9},{9,8},{10,11... | collective-permute-start | bytes 1572872 | tf_op jit(solution)/shard_map/ppermute | solution.py:396
  14.0 5.5 %copy-start.2 = (s32[1,1024]{1,0:T(1,128)S(1)}, s32[1,1024]{1,0:T(1,128)}, u32[]{:S(2)}) copy-start(s32[1,1024]{1,0:T(1,128)} %refs_9_.1) | copy-start | bytes 12292
  19.8 15.1 %copy-start.1 = (s32[1024,1]{1,0:T(8,128)}, s32[1024,1]{1,0:T(8,128)S(1)}, u32[]{:S(2)}) copy-start(s32[1024,1]{1,0:T(8,128)S(1)} %copy.25.ids_col.refs_8_) | copy-start | bytes 12292
  19.8 15.1 %copy-start.3 = (bf16[1024,512]{1,0:T(8,128)(2,1)S(1)}, bf16[1024,512]{1,0:T(8,128)(2,1)}, u32[]{:S(2)}) copy-start(bf16[1024,512]{1,0:T(8,128)(2,1)} %refs_5_.1) | copy-start | bytes 3145732
  19.8 15.0 %copy-start.4 = (bf16[1024,512]{1,0:T(8,128)(2,1)S(1)}, bf16[1024,512]{1,0:T(8,128)(2,1)}, u32[]{:S(2)}) copy-start(bf16[1024,512]{1,0:T(8,128)(2,1)} %refs_6_.1) | copy-start | bytes 3145732
  19.8 15.0 %copy-start.5 = (bf16[1,1024,512]{2,1,0:T(8,128)(2,1)S(1)}, bf16[1,1024,512]{2,1,0:T(8,128)(2,1)}, u32[]{:S(2)}) copy-start(bf16[1,1024,512]{2,1,0:T(8,128)(2,1)} %param.24) | copy-start | bytes 3145732
  25.0 23.2 %copy-start.7 = (bf16[1024,512]{1,0:T(8,128)(2,1)}, bf16[1024,512]{1,0:T(8,128)(2,1)S(1)}, u32[]{:S(2)}) copy-start(bf16[1024,512]{1,0:T(8,128)(2,1)S(1)} %get-tuple-element.17.query_w.refs_4_) | copy-start | bytes 3145732
  34.9 13.4 %copy-start.6 = (bf16[256,1024]{1,0:T(8,128)(2,1)}, bf16[256,1024]{1,0:T(8,128)(2,1)S(1)}, u32[]{:S(2)}) copy-start(bf16[256,1024]{1,0:T(8,128)(2,1)S(1)} %collective-permute-done.2.near.refs_1_) | copy-start | bytes 1572868
  48.3 0.8 copy-start.8
  49.1 37.0 %copy-start.10 = (bf16[1,1024,512]{2,1,0:T(8,128)(2,1)S(1)}, bf16[1,1024,512]{2,1,0:T(8,128)(2,1)}, u32[]{:S(2)}) copy-start(bf16[1,1024,512]{2,1,0:T(8,128)(2,1)} %param.18) | copy-start | bytes 3145732
